TPU v7x, 512 devices: a whole 4x8x8 slice. The times are simulated.
512 devices in a mesh: gx: 64 (over x, y, core), ta: 8 (over z).
Axes of the slice: x: 4, y: 8, z: 8, core: 2. Of those that a mesh axis runs over, the one named last changes fastest.
Arguments:
- master_flat: float32 [8388608], P(('gx', 'ta')), may hold values from -6 to 6
Outputs:
- serving_weight: bfloat16 [1, 8192, 1024], P(None, None, 'ta')
- channel_scale: float32 [1, 1024], P(None, 'ta')
All inputs are finite; a program needn't handle non-finite values.
Results may differ from a plain program's by a relative error of at most 0.015.
Values may be sent and summed in bfloat16 or wider, within the bound.
A program may use at most 64 MiB of HBM per device.

v0:
```python
import jax
import jax.numpy as jnp
from jax import lax
from jax.sharding import PartitionSpec as P

D = 8192
KVH = 8
HEAD = 128
LAYERS = 1


def relayout(shard):
    regrouped = lax.all_to_all(shard, "ta", split_axis=1, concat_axis=0, tiled=True)
    complete = lax.all_gather(regrouped, "gx", axis=0, tiled=True)
    return complete.reshape(LAYERS, D, -1)


def shards(master_flat):
    kv_width = KVH * HEAD
    row_count = master_flat.shape[0] // kv_width
    rounded = master_flat.reshape(row_count, kv_width).astype(jnp.bfloat16)
    complete = relayout(rounded)
    widened = complete.astype(jnp.float32)
    channel_scale = jnp.max(jnp.abs(widened), axis=1)
    serving_weight = (widened / channel_scale[:, None, :]).astype(jnp.bfloat16)
    return (serving_weight, channel_scale)


def solution(mesh):
    in_specs = (P(("gx", "ta")),)
    out_specs = (P(None, None, "ta"), P(None, "ta"))
    return jax.shard_map(shards, mesh=mesh, in_specs=in_specs, out_specs=out_specs, check_vma=False)
```

profile of v0, /device:TPU:1, one launch (start us, length us, event | category | flops | bytes accessed | tf_op | source)
XLA Modules:
  0.0 117.4 jit_solution(15112434270394180846)
XLA Ops:
  7.2 0.0 all-gather.2.cloned.1.call-start
  7.2 0.8 convert_bitcast_fusion
  8.1 17.5 %all_to_all.16 = bf16[16,8,128]{2,0,1:T(8,128)(2,1)} all-to-all(bf16[16,8,128]{2,0,1:T(8,128)(2,1)S(1)} %copy.4), channel_id=1, replica_groups=mesh['gx'=64,'ta'=8] {'ta'}, dimensions={1} | all-to-all | bytes 65536 | tf_op jit(solution)/shard_map/all_to_all | solution.py:13
  25.5 0.0 all-gather.2.cloned.1.call-update
  25.6 81.0 %all-gather.2.cloned.1.call-done = bf16[8192,128]{1,0:T(8,128)(2,1)} async-done(((bf16[128,128]{1,0:T(8,128)(2,1)}), bf16[8192,128]{1,0:T(8,128)(2,1)}) %all-gather.2.cloned.1.call-update) | async-done | bytes 2097168 | tf_op jit(solution)/shard_map/all_gather | solution.py:14
  106.6 0.0 copy-start
  106.6 2.0 %fusion = f32[128]{0:T(128)S(1)} fusion(bf16[8192,128]{1,0:T(8,128)(2,1)} %all-gather.2.cloned.1.call-done), kind=kLoop, calls=%fused_computation.2 | loop fusion | flops 3145600 | bytes 2097664 | tf_op jit(solution)/shard_map/reduce_max | solution.py:24
  108.6 0.2 copy-done
  108.8 0.0 copy-start.1
  108.8 1.7 %fusion.2 = bf16[1,8192,128]{2,1,0:T(8,128)(2,1)} fusion(bf16[8192,128]{1,0:T(8,128)(2,1)S(1)} %copy-done, f32[128]{0:T(128)S(1)} %fusion), kind=kLoop, calls=%fused_computation.4 | loop fusion | flops 3145728 | bytes 4194816 | tf_op jit(solution)/shard_map/convert_element_type | solution.py:25
  110.5 0.0 copy-done.1
  (1 shorter events, 0.0 us)
Async XLA Ops:
  7.2 99.4 %all-gather.2.cloned.1.call-start = ((), (), s32[]{:S(2)}) async-start(), calls=%async_computation.1 | async-start | bytes 2129920 | tf_op jit(solution)/shard_map/all_gather | solution.py:14
  106.6 2.2 %copy-start = (bf16[8192,128]{1,0:T(8,128)(2,1)S(1)}, bf16[8192,128]{1,0:T(8,128)(2,1)}, u32[]{:S(2)}) copy-start(bf16[8192,128]{1,0:T(8,128)(2,1)} %all-gather.2.cloned.1.call-done) | copy-start | bytes 6291460
  108.8 1.7 %copy-start.1 = (f32[128]{0:T(128)}, f32[128]{0:T(128)S(1)}, u32[]{:S(2)}) copy-start(f32[128]{0:T(128)S(1)} %fusion) | copy-start | bytes 1540
Sparse Core Ops, SparseCore 0:
  25.7 80.8 all-gather.1
where the time goes:
time: 118 us; the launch traced here: 117 us
  waiting for transfers between devices  81 us (69%)
  blocking collectives  17.5 us (15%)
  between operations  14 us (12%)
  other arithmetic  4.6 us (4%)
    all_gather x1, waiting for transfers between devices, relayout(): complete = lax.all_gather(regrouped, 'gx', axis=0, tiled=True)  81 us
    all_to_all x1, blocking collectives, relayout(): lax.all_to_all(shard, 'ta', split_axis=1, concat_axis=0, tiled=True)  17.5 us
  transfers between devices with their start and end apart: 1, of which 1 were waited for; matrix products, arithmetic and copies ran while one was open for 0% of the time, Pallas kernels for 0%

commit v1 on v0

v1 whole, which is shorter than its diff:
```python
import functools

import jax
import jax.numpy as jnp
from jax import lax
from jax.experimental import pallas as pl
from jax.experimental.pallas import tpu as pltpu
from jax.sharding import PartitionSpec as P

D = 8192
HEADS_WIDTH = 128
X, Y, Z = 4, 8, 8
ROWS = 16
HALF = Z * ROWS
FIRST = 3 * ROWS
MESH = pl.DeviceIdType.MESH


def order_of(step, size):
    return lax.rem(jnp.where(step % 2 == 1, (step + 1) // 2, size - step // 2), size)


def gather_kernel(x_hbm, out_ref, stage, rounded, load_sem, swap_send, swap_recv, send_sem, a_recv, b_recv, core_send, core_recv):
    gx, z = lax.axis_index("gx"), lax.axis_index("ta")
    core, chip = lax.rem(gx, 2), gx // 2
    x, y = chip // Y, lax.rem(chip, Y)

    load = pltpu.make_async_copy(x_hbm, stage, load_sem)
    load.start()

    barrier = pltpu.get_barrier_semaphore()

    def device(xt, yt, zt, ct):
        return ((xt * Y + yt) * 2 + ct, zt)

    def greet(xt, yt, zt, ct):
        pl.semaphore_signal(barrier, inc=1, device_id=device(xt, yt, zt, ct), device_id_type=MESH)

    greet(x, y, z, 1 - core)
    for d in range(1, Z):
        greet(x, y, lax.rem(z + d, Z), core)
    for d in range(1, Y):
        greet(x, lax.rem(y + d, Y), z, core)
    for d in range(1, X):
        greet(lax.rem(x + d, X), y, z, core)

    def rows_of(xt, yt, ct, offset, count):
        start = ((xt * Y + yt) * 2 + ct) * HALF + offset
        return pl.ds(pl.multiple_of(start, ROWS), count)

    load.wait()
    for k in range(Z):
        rounded[k] = stage[pl.ds(k, ROWS, stride=Z), :].astype(jnp.bfloat16)
    out_ref[rows_of(x, y, core, z * ROWS, ROWS), :] = rounded[z]

    pl.semaphore_wait(barrier, 1 + (Z - 1) + (Y - 1) + (X - 1))

    def remote(src, dst, send, recv, to):
        return pltpu.make_async_remote_copy(src_ref=src, dst_ref=dst, send_sem=send, recv_sem=recv, device_id=to, device_id_type=MESH)

    here = out_ref.at[rows_of(x, y, core, z * ROWS, ROWS)]
    for d in (4, 3, 5, 2, 6, 1, 7):
        to = lax.rem(z + d, Z)
        remote(rounded.at[to], here, swap_send, swap_recv, device(x, y, to, core)).start()

    def along_y(ref, recv):
        for d in (4, 3, 5, 2, 6, 1, 7):
            remote(ref, ref, send_sem, recv, device(x, lax.rem(y + d, Y), z, core)).start()

    def along_x(ref, recv):
        for d in (2, 1, 3):
            remote(ref, ref, send_sem, recv, device(lax.rem(x + d, X), y, z, core)).start()

    def across(ref):
        remote(ref, ref, core_send, core_recv, device(x, y, z, 1 - core)).start()

    def part_a(xt, yt):
        return out_ref.at[rows_of(xt, yt, core, 0, FIRST)]

    def part_b(xt, yt):
        return out_ref.at[rows_of(xt, yt, core, FIRST, HALF - FIRST)]

    def whole(xt, yt):
        return out_ref.at[rows_of(xt, yt, core, 0, HALF)]

    def waiter(ref, sem):
        pltpu.make_async_copy(ref, ref, sem).wait()

    others = out_ref.at[pl.ds(0, (Z - 1) * ROWS)]
    waiter(others, swap_recv)
    along_x(part_a(x, y), a_recv.at[chip])
    along_y(part_b(x, y), b_recv.at[chip])
    along_y(part_a(x, y), a_recv.at[chip])
    along_x(part_b(x, y), b_recv.at[chip])
    across(whole(x, y))

    def arrival(step, carry):
        xt = order_of(step // 8, X)
        yt = order_of(lax.rem(step, 8), Y)
        source = xt * Y + yt

        @pl.when(source != chip)
        def _():
            waiter(part_a(xt, yt), a_recv.at[source])

            @pl.when(yt == y)
            def _():
                along_y(part_a(xt, yt), a_recv.at[source])

            waiter(part_b(xt, yt), b_recv.at[source])

            @pl.when(xt == x)
            def _():
                along_x(part_b(xt, yt), b_recv.at[source])

            across(whole(xt, yt))

        return carry

    lax.fori_loop(0, X * Y, arrival, 0)

    waiter(out_ref.at[pl.ds(0, D // 2)], core_recv)
    waiter(others, swap_send)
    sent = X * FIRST * (Y - 1) + (X - 1) * FIRST + Y * (HALF - FIRST) * (X - 1) + (Y - 1) * (HALF - FIRST)
    waiter(out_ref.at[pl.ds(0, sent)], send_sem)
    waiter(out_ref.at[pl.ds(0, D // 2)], core_send)


TILE = 1024


def scale_kernel(w_ref, out_hbm, scale_hbm, buffer, scale_vmem, out_sem, scale_sem):
    def step(i, best):
        block = jnp.abs(w_ref[pl.ds(pl.multiple_of(i * 256, 256), 256), :])
        return jnp.maximum(best, jnp.max(block.reshape(8, 32, HEADS_WIDTH), axis=0))

    best = lax.fori_loop(0, D // 256, step, jnp.zeros((32, HEADS_WIDTH), jnp.bfloat16))
    scale = jnp.max(best.astype(jnp.float32), axis=0, keepdims=True)
    scale_vmem[...] = scale
    scale_out = pltpu.make_async_copy(scale_vmem, scale_hbm, scale_sem)
    scale_out.start()
    inverse = jnp.broadcast_to(1.0 / scale, (64, HEADS_WIDTH))
    copies = []
    for t in range(D // TILE):
        def scaled(i, carry):
            rows = pl.ds(pl.multiple_of(t * TILE + i * 64, 64), 64)
            buffer[rows, :] = (w_ref[rows, :].astype(jnp.float32) * inverse).astype(jnp.bfloat16)
            return carry

        lax.fori_loop(0, TILE // 64, scaled, 0, unroll=4)
        rows = pl.ds(t * TILE, TILE)
        copies.append(pltpu.make_async_copy(buffer.at[rows], out_hbm.at[rows], out_sem.at[t]))
        copies[-1].start()
    for copy in copies:
        copy.wait()
    scale_out.wait()


def shards(master_flat):
    flat = master_flat.reshape(ROWS * Z, HEADS_WIDTH)
    gathered = pl.pallas_call(
        gather_kernel,
        name="gather",
        out_shape=jax.ShapeDtypeStruct((D, HEADS_WIDTH), jnp.bfloat16),
        in_specs=[pl.BlockSpec(memory_space=pltpu.HBM)],
        out_specs=pl.BlockSpec(memory_space=pltpu.VMEM),
        scratch_shapes=[
            pltpu.VMEM((ROWS * Z, HEADS_WIDTH), jnp.float32),
            pltpu.VMEM((Z, ROWS, HEADS_WIDTH), jnp.bfloat16),
            pltpu.SemaphoreType.DMA,
            pltpu.SemaphoreType.DMA,
            pltpu.SemaphoreType.DMA,
            pltpu.SemaphoreType.DMA,
            pltpu.SemaphoreType.DMA((X * Y,)),
            pltpu.SemaphoreType.DMA((X * Y,)),
            pltpu.SemaphoreType.DMA,
            pltpu.SemaphoreType.DMA,
        ],
        compiler_params=pltpu.CompilerParams(collective_id=0, has_side_effects=True, vmem_limit_bytes=16 * 1024 * 1024),
    )(flat)
    weight, scale = pl.pallas_call(
        scale_kernel,
        name="scale",
        out_shape=(jax.ShapeDtypeStruct((D, HEADS_WIDTH), jnp.bfloat16), jax.ShapeDtypeStruct((1, HEADS_WIDTH), jnp.float32)),
        in_specs=[pl.BlockSpec(memory_space=pltpu.VMEM)],
        out_specs=(pl.BlockSpec(memory_space=pl.ANY), pl.BlockSpec(memory_space=pl.ANY)),
        scratch_shapes=[
            pltpu.VMEM((D, HEADS_WIDTH), jnp.bfloat16),
            pltpu.VMEM((1, HEADS_WIDTH), jnp.float32),
            pltpu.SemaphoreType.DMA((D // TILE,)),
            pltpu.SemaphoreType.DMA,
        ],
        compiler_params=pltpu.CompilerParams(vmem_limit_bytes=16 * 1024 * 1024),
    )(gathered)
    return weight.reshape(1, D, HEADS_WIDTH), scale


def solution(mesh):
    return jax.shard_map(shards, mesh=mesh, in_specs=(P(("gx", "ta")),), out_specs=(P(None, None, "ta"), P(None, "ta")), check_vma=False)
```

time: 118 us -> 158 us (1.34)
  Pallas kernels: 0 us -> 156 us
  waiting for transfers between devices: 81 us -> 0 us
  blocking collectives: 17.5 us -> 0 us
  between operations: 14 us -> 0.65 us
  other arithmetic: 4.6 us -> 0 us
    pallas_call x0 -> x2, Pallas kernels: none -> 156 us  [the longest x1 154 us: shards(): pl.pallas_call(gather_kernel, name='gather', out_shape=jax.ShapeDtypeStru...]
    all_gather x1 -> x0, waiting for transfers between devices: 81 us -> none  [relayout(): complete = lax.all_gather(regrouped, 'gx', axis=0, tiled=True)]
    all_to_all x1 -> x0, blocking collectives: 17.5 us -> none  [relayout(): lax.all_to_all(shard, 'ta', split_axis=1, concat_axis=0, tiled=True)]
    convert_element_type x2 -> x0, other arithmetic: 2.57 us -> none  [the longest x1 1.73 us: shards(): serving_weight = (widened / channel_scale[:, None, :]).astype(jnp.bfloat16)]
    reduce_max x1 -> x0, other arithmetic: 2.03 us -> none  [shards(): channel_scale = jnp.max(jnp.abs(widened), axis=1)]
  transfers between devices with their start and end apart: 1 -> 0, of which waited for: 1 -> 0; matrix products, arithmetic and copies ran while one was open for 0% -> 0% of each run, Pallas kernels for 0% -> 0%
where the time goes in v1:
time: 158 us
  Pallas kernels  156 us (99%)
    pallas_call x1, Pallas kernels, shards(): pl.pallas_call(gather_kernel, name='gather', out_shape=jax.ShapeDtypeStru...  154 us

profile of v1, /device:TPU:1, one launch (start us, length us, event | category | flops | bytes accessed | tf_op | source)
XLA Modules:
  0.0 157.9 jit_solution(9901428120120466934)
XLA Ops:
  0.6 0.0 copy-start
  0.6 0.8 copy-done
  1.5 154.1 %gather.1.w_ref = bf16[8192,128]{1,0:T(8,128)(2,1)S(1)} custom-call(f32[128,128]{1,0:T(8,128)S(1)} %bitcast.2), custom_call_target="tpu_custom_call" | custom-call | tf_op jit(solution)/shard_map/gather/pallas_call | solution.py:161
  155.6 2.3 %scale.1 = (bf16[8192,128]{1,0:T(8,128)(2,1)}, f32[1,128]{1,0:T(1,128)}) custom-call(bf16[8192,128]{1,0:T(8,128)(2,1)S(1)} %gather.1.w_ref), custom_call_target="tpu_custom_call" | custom-call | tf_op jit(solution)/shard_map/scale/pallas_call | solution.py:181
Async XLA Ops:
  0.6 0.8 copy-start

commit v2 on v1

--- a/solution.py
+++ b/solution.py
@@ -12,7 +12,7 @@
 X, Y, Z = 4, 8, 8
 ROWS = 16
 HALF = Z * ROWS
-FIRST = 3 * ROWS
+FIRST = 2 * ROWS
 MESH = pl.DeviceIdType.MESH
 
 
@@ -94,6 +94,34 @@
     along_x(part_b(x, y), b_recv.at[chip])
     across(whole(x, y))
 
+    def from_x(step, carry):
+        xt = order_of(step, X)
+
+        @pl.when(xt != x)
+        def _():
+            source = xt * Y + y
+            waiter(part_a(xt, y), a_recv.at[source])
+            along_y(part_a(xt, y), a_recv.at[source])
+
+        return carry
+
+    def from_y(step, carry):
+        yt = order_of(step, Y)
+
+        @pl.when(yt != y)
+        def _():
+            source = x * Y + yt
+            waiter(part_b(x, yt), b_recv.at[source])
+            along_x(part_b(x, yt), b_recv.at[source])
+
+        return carry
+
+    lax.fori_loop(0, 2, from_y, 0)
+    lax.fori_loop(0, 2, from_x, 0)
+    lax.fori_loop(2, 5, from_y, 0)
+    lax.fori_loop(2, X, from_x, 0)
+    lax.fori_loop(5, Y, from_y, 0)
+
     def arrival(step, carry):
         xt = order_of(step // 8, X)
         yt = order_of(lax.rem(step, 8), Y)
@@ -101,17 +129,13 @@
 
         @pl.when(source != chip)
         def _():
-            waiter(part_a(xt, yt), a_recv.at[source])
-
-            @pl.when(yt == y)
+            @pl.when(yt != y)
             def _():
-                along_y(part_a(xt, yt), a_recv.at[source])
-
-            waiter(part_b(xt, yt), b_recv.at[source])
-
-            @pl.when(xt == x)
+                waiter(part_a(xt, yt), a_recv.at[source])
+
+            @pl.when(xt != x)
             def _():
-                along_x(part_b(xt, yt), b_recv.at[source])
+                waiter(part_b(xt, yt), b_recv.at[source])
 
             across(whole(xt, yt))
 
@@ -157,7 +181,7 @@
 
 
 def shards(master_flat):
-    flat = master_flat.reshape(ROWS * Z, HEADS_WIDTH)
+    flat = pltpu.with_memory_space_constraint(master_flat.reshape(ROWS * Z, HEADS_WIDTH), pltpu.HBM)
     gathered = pl.pallas_call(
         gather_kernel,
         name="gather",

time: 158 us -> 39.2 us (0.25)
  Pallas kernels: 156 us -> 38.4 us
    pallas_call x1, Pallas kernels: 154 us -> 36.1 us  [shards(): pl.pallas_call(gather_kernel, name='gather', out_shape=jax.ShapeDtypeStru...]
where the time goes in v2:
time: 39.2 us; the launch traced here: 39.1 us
  Pallas kernels  38.4 us (98%)
  between operations  0.64 us (2%)
    pallas_call x1, Pallas kernels, shards(): pl.pallas_call(gather_kernel, name='gather', out_shape=jax.ShapeDtypeStru...  36.1 us
    pallas_call x1, Pallas kernels, shards(): pl.pallas_call(scale_kernel, name='scale', out_shape=(jax.ShapeDtypeStruc...  2.3 us

profile of v2, /device:TPU:1, one launch (start us, length us, event | category | flops | bytes accessed | tf_op | source)
XLA Modules:
  0.0 39.1 jit_solution(782211645479535188)
XLA Ops:
  0.6 36.1 %gather.1.w_ref = bf16[8192,128]{1,0:T(8,128)(2,1)S(1)} custom-call(f32[128,128]{1,0:T(8,128)} %bitcast.2), custom_call_target="tpu_custom_call" | custom-call | tf_op jit(solution)/shard_map/gather/pallas_call | solution.py:185
  36.8 2.3 %scale.1 = (bf16[8192,128]{1,0:T(8,128)(2,1)}, f32[1,128]{1,0:T(1,128)}) custom-call(bf16[8192,128]{1,0:T(8,128)(2,1)S(1)} %gather.1.w_ref), custom_call_target="tpu_custom_call" | custom-call | tf_op jit(solution)/shard_map/scale/pallas_call | solution.py:205

commit v3 on v1

--- a/solution.py
+++ b/solution.py
@@ -12,18 +12,23 @@
 X, Y, Z = 4, 8, 8
 ROWS = 16
 HALF = Z * ROWS
-FIRST = 3 * ROWS
+A_END, LATE = 2, 5
 MESH = pl.DeviceIdType.MESH
+
+
+def rank(at, size):
+    return jnp.where(at * 2 <= size, jnp.maximum(2 * at - 1, 0), 2 * (size - at))
 
 
 def order_of(step, size):
     return lax.rem(jnp.where(step % 2 == 1, (step + 1) // 2, size - step // 2), size)
 
 
-def gather_kernel(x_hbm, out_ref, stage, rounded, load_sem, swap_send, swap_recv, send_sem, a_recv, b_recv, core_send, core_recv):
+def gather_kernel(x_hbm, out_ref, stage, rounded, load_sem, entered_z, entered, swap_send, swap_recv, send_sem, a_recv, b_recv, late_recv, core_send, core_recv):
     gx, z = lax.axis_index("gx"), lax.axis_index("ta")
     core, chip = lax.rem(gx, 2), gx // 2
     x, y = chip // Y, lax.rem(chip, Y)
+    x_rank, y_rank = rank(x, X), rank(y, Y)
 
     load = pltpu.make_async_copy(x_hbm, stage, load_sem)
     load.start()
@@ -33,35 +38,83 @@
     def device(xt, yt, zt, ct):
         return ((xt * Y + yt) * 2 + ct, zt)
 
-    def greet(xt, yt, zt, ct):
-        pl.semaphore_signal(barrier, inc=1, device_id=device(xt, yt, zt, ct), device_id_type=MESH)
-
-    greet(x, y, z, 1 - core)
-    for d in range(1, Z):
-        greet(x, y, lax.rem(z + d, Z), core)
-    for d in range(1, Y):
-        greet(x, lax.rem(y + d, Y), z, core)
-    for d in range(1, X):
-        greet(lax.rem(x + d, X), y, z, core)
+    def signal(semaphore, to):
+        pl.semaphore_signal(semaphore, inc=1, device_id=to, device_id_type=MESH)
+
+    def around(size, at, then):
+        for d in range(1, size):
+            then(lax.rem(at + d, size))
+
+    def greet(later, to):
+        @pl.when(later)
+        def _():
+            signal(barrier, to)
+
+    greet(core == 1, device(x, y, z, 1 - core))
+    around(Z, z, lambda zt: greet(zt > z, device(x, y, zt, core)))
+    around(Y, y, lambda yt: greet(rank(yt, Y) > y_rank, device(x, yt, z, core)))
+    around(X, x, lambda xt: greet(rank(xt, X) > x_rank, device(xt, y, z, core)))
 
     def rows_of(xt, yt, ct, offset, count):
         start = ((xt * Y + yt) * 2 + ct) * HALF + offset
         return pl.ds(pl.multiple_of(start, ROWS), count)
 
+    def wait_for(semaphore, count):
+        @pl.when(count > 0)
+        def _():
+            pl.semaphore_wait(semaphore, count)
+
+    wait_for(barrier, (1 - core) + z + y_rank + x_rank)
+
+    def answer(earlier, semaphore, to):
+        @pl.when(earlier)
+        def _():
+            signal(semaphore, to)
+
+    around(Z, z, lambda zt: answer(zt < z, entered_z.at[z], device(x, y, zt, core)))
+    around(Y, y, lambda yt: answer(rank(yt, Y) < y_rank, entered, device(x, yt, z, core)))
+    around(X, x, lambda xt: answer(rank(xt, X) < x_rank, entered, device(xt, y, z, core)))
+    answer(core == 0, entered, device(x, y, z, 1 - core))
+
     load.wait()
     for k in range(Z):
         rounded[k] = stage[pl.ds(k, ROWS, stride=Z), :].astype(jnp.bfloat16)
-    out_ref[rows_of(x, y, core, z * ROWS, ROWS), :] = rounded[z]
-
-    pl.semaphore_wait(barrier, 1 + (Z - 1) + (Y - 1) + (X - 1))
+    here = rows_of(x, y, core, z * ROWS, ROWS)
+    out_ref[here, :] = rounded[z]
 
     def remote(src, dst, send, recv, to):
         return pltpu.make_async_remote_copy(src_ref=src, dst_ref=dst, send_sem=send, recv_sem=recv, device_id=to, device_id_type=MESH)
 
-    here = out_ref.at[rows_of(x, y, core, z * ROWS, ROWS)]
-    for d in (4, 3, 5, 2, 6, 1, 7):
-        to = lax.rem(z + d, Z)
-        remote(rounded.at[to], here, swap_send, swap_recv, device(x, y, to, core)).start()
+    def swap(zt):
+        @pl.when(zt > z)
+        def _():
+            pl.semaphore_wait(entered_z.at[zt], 1)
+
+        remote(rounded.at[zt], out_ref.at[here], swap_send, swap_recv.at[z], device(x, y, zt, core)).start()
+
+    def swap_soon(zt, carry):
+        @pl.when((zt != z) & ((zt < z) | (zt < LATE)))
+        def _():
+            swap(zt)
+
+        return carry
+
+    def swap_rest(zt, carry):
+        @pl.when(zt > z)
+        def _():
+            swap(zt)
+
+        return carry
+
+    def waiter(ref, sem):
+        pltpu.make_async_copy(ref, ref, sem).wait()
+
+    def swapped(zt, carry):
+        @pl.when(zt != z)
+        def _():
+            waiter(rounded.at[zt], swap_recv.at[zt])
+
+        return carry
 
     def along_y(ref, recv):
         for d in (4, 3, 5, 2, 6, 1, 7):
@@ -75,53 +128,89 @@
         remote(ref, ref, core_send, core_recv, device(x, y, z, 1 - core)).start()
 
     def part_a(xt, yt):
-        return out_ref.at[rows_of(xt, yt, core, 0, FIRST)]
+        return out_ref.at[rows_of(xt, yt, core, 0, A_END * ROWS)]
 
     def part_b(xt, yt):
-        return out_ref.at[rows_of(xt, yt, core, FIRST, HALF - FIRST)]
-
-    def whole(xt, yt):
-        return out_ref.at[rows_of(xt, yt, core, 0, HALF)]
-
-    def waiter(ref, sem):
-        pltpu.make_async_copy(ref, ref, sem).wait()
-
-    others = out_ref.at[pl.ds(0, (Z - 1) * ROWS)]
-    waiter(others, swap_recv)
+        return out_ref.at[rows_of(xt, yt, core, A_END * ROWS, (LATE - A_END) * ROWS)]
+
+    def part_late(xt, yt):
+        return out_ref.at[rows_of(xt, yt, core, LATE * ROWS, (Z - LATE) * ROWS)]
+
+    def early(xt, yt):
+        return out_ref.at[rows_of(xt, yt, core, 0, LATE * ROWS)]
+
+    lax.fori_loop(0, Z, swap_soon, 0)
+    lax.fori_loop(0, A_END, swapped, 0)
+    wait_for(entered, (Y - 1 - y_rank) + (X - 1 - x_rank) + core)
     along_x(part_a(x, y), a_recv.at[chip])
+    along_y(part_a(x, y), a_recv.at[chip])
+    lax.fori_loop(A_END, LATE, swapped, 0)
     along_y(part_b(x, y), b_recv.at[chip])
-    along_y(part_a(x, y), a_recv.at[chip])
     along_x(part_b(x, y), b_recv.at[chip])
-    across(whole(x, y))
+    across(early(x, y))
+    lax.fori_loop(LATE, Z, swap_rest, 0)
+    lax.fori_loop(LATE, Z, swapped, 0)
+    along_y(part_late(x, y), late_recv.at[chip])
+    along_x(part_late(x, y), late_recv.at[chip])
+    across(part_late(x, y))
+
+    def forward(part, recv, step, over_x):
+        xt, yt = (order_of(step, X), y) if over_x else (x, order_of(step, Y))
+
+        @pl.when((xt != x) | (yt != y))
+        def _():
+            ref, sem = part(xt, yt), recv.at[xt * Y + yt]
+            waiter(ref, sem)
+            (along_y if over_x else along_x)(ref, sem)
+
+        return 0
+
+    from_x = lambda step, carry: forward(part_a, a_recv, step, True)
+    from_y = lambda step, carry: forward(part_b, b_recv, step, False)
+    late_from_y = lambda step, carry: forward(part_late, late_recv, step, False)
+    lax.fori_loop(0, X, from_x, 0)
+    lax.fori_loop(0, Y, from_y, 0)
+    lax.fori_loop(0, Y, late_from_y, 0)
 
     def arrival(step, carry):
-        xt = order_of(step // 8, X)
-        yt = order_of(lax.rem(step, 8), Y)
+        xt, yt = order_of(step // 8, X), order_of(lax.rem(step, 8), Y)
         source = xt * Y + yt
 
         @pl.when(source != chip)
         def _():
-            waiter(part_a(xt, yt), a_recv.at[source])
-
-            @pl.when(yt == y)
+            @pl.when(yt != y)
             def _():
-                along_y(part_a(xt, yt), a_recv.at[source])
-
-            waiter(part_b(xt, yt), b_recv.at[source])
-
-            @pl.when(xt == x)
+                waiter(part_a(xt, yt), a_recv.at[source])
+
+            @pl.when(xt != x)
             def _():
-                along_x(part_b(xt, yt), b_recv.at[source])
-
-            across(whole(xt, yt))
+                waiter(part_b(xt, yt), b_recv.at[source])
+
+            across(early(xt, yt))
+
+        return carry
+
+    def late_arrival(step, carry):
+        xt, yt = order_of(step // 8, X), order_of(lax.rem(step, 8), Y)
+        source = xt * Y + yt
+
+        @pl.when(source != chip)
+        def _():
+            @pl.when(xt != x)
+            def _():
+                waiter(part_late(xt, yt), late_recv.at[source])
+
+            across(part_late(xt, yt))
 
         return carry
 
     lax.fori_loop(0, X * Y, arrival, 0)
+    lax.fori_loop(0, X * Y, late_arrival, 0)
 
     waiter(out_ref.at[pl.ds(0, D // 2)], core_recv)
-    waiter(others, swap_send)
-    sent = X * FIRST * (Y - 1) + (X - 1) * FIRST + Y * (HALF - FIRST) * (X - 1) + (Y - 1) * (HALF - FIRST)
+    waiter(out_ref.at[pl.ds(0, (Z - 1) * ROWS)], swap_send)
+    a_rows, b_rows = A_END * ROWS, (Z - A_END) * ROWS
+    sent = a_rows * ((X - 1) + X * (Y - 1)) + b_rows * ((Y - 1) + Y * (X - 1))
     waiter(out_ref.at[pl.ds(0, sent)], send_sem)
     waiter(out_ref.at[pl.ds(0, D // 2)], core_send)
 
@@ -157,7 +246,7 @@
 
 
 def shards(master_flat):
-    flat = master_flat.reshape(ROWS * Z, HEADS_WIDTH)
+    flat = pltpu.with_memory_space_constraint(master_flat.reshape(ROWS * Z, HEADS_WIDTH), pltpu.HBM)
     gathered = pl.pallas_call(
         gather_kernel,
         name="gather",
@@ -168,9 +257,12 @@
             pltpu.VMEM((ROWS * Z, HEADS_WIDTH), jnp.float32),
             pltpu.VMEM((Z, ROWS, HEADS_WIDTH), jnp.bfloat16),
             pltpu.SemaphoreType.DMA,
-            pltpu.SemaphoreType.DMA,
-            pltpu.SemaphoreType.DMA,
-            pltpu.SemaphoreType.DMA,
+            pltpu.SemaphoreType.REGULAR((Z,)),
+            pltpu.SemaphoreType.REGULAR,
+            pltpu.SemaphoreType.DMA,
+            pltpu.SemaphoreType.DMA((Z,)),
+            pltpu.SemaphoreType.DMA,
+            pltpu.SemaphoreType.DMA((X * Y,)),
             pltpu.SemaphoreType.DMA((X * Y,)),
             pltpu.SemaphoreType.DMA((X * Y,)),
             pltpu.SemaphoreType.DMA,

time: 158 us -> 35.7 us (0.23)
  Pallas kernels: 156 us -> 34.9 us
    pallas_call x1, Pallas kernels: 154 us -> 32.6 us  [shards(): pl.pallas_call(gather_kernel, name='gather', out_shape=jax.ShapeDtypeStru...]
where the time goes in v3:
time: 35.7 us; the launch traced here: 35.5 us
  Pallas kernels  34.9 us (98%)
  between operations  0.64 us (2%)
    pallas_call x1, Pallas kernels, shards(): pl.pallas_call(gather_kernel, name='gather', out_shape=jax.ShapeDtypeStru...  32.6 us
    pallas_call x1, Pallas kernels, shards(): pl.pallas_call(scale_kernel, name='scale', out_shape=(jax.ShapeDtypeStruc...  2.3 us

profile of v3, /device:TPU:1, one launch (start us, length us, event | category | flops | bytes accessed | tf_op | source)
XLA Modules:
  0.0 35.5 jit_solution(18377570477580793110)
XLA Ops:
  0.6 32.6 %gather.1.w_ref = bf16[8192,128]{1,0:T(8,128)(2,1)S(1)} custom-call(f32[128,128]{1,0:T(8,128)} %bitcast.2), custom_call_target="tpu_custom_call" | custom-call | tf_op jit(solution)/shard_map/gather/pallas_call | solution.py:250
  33.2 2.3 %scale.1 = (bf16[8192,128]{1,0:T(8,128)(2,1)}, f32[1,128]{1,0:T(1,128)}) custom-call(bf16[8192,128]{1,0:T(8,128)(2,1)S(1)} %gather.1.w_ref), custom_call_target="tpu_custom_call" | custom-call | tf_op jit(solution)/shard_map/scale/pallas_call | solution.py:273

commit v4 on v3

--- a/solution.py
+++ b/solution.py
@@ -12,7 +12,7 @@
 X, Y, Z = 4, 8, 8
 ROWS = 16
 HALF = Z * ROWS
-A_END, LATE = 2, 5
+A_END, LATE = 2, 4
 MESH = pl.DeviceIdType.MESH
 
 
@@ -24,7 +24,7 @@
     return lax.rem(jnp.where(step % 2 == 1, (step + 1) // 2, size - step // 2), size)
 
 
-def gather_kernel(x_hbm, out_ref, stage, rounded, load_sem, entered_z, entered, swap_send, swap_recv, send_sem, a_recv, b_recv, late_recv, core_send, core_recv):
+def gather_kernel(x_hbm, out_ref, scale_ref, stage, rounded, load_sem, entered_z, entered, swap_send, swap_recv, send_sem, a_recv, b_recv, late_recv, core_send, core_recv, core_late):
     gx, z = lax.axis_index("gx"), lax.axis_index("ta")
     core, chip = lax.rem(gx, 2), gx // 2
     x, y = chip // Y, lax.rem(chip, Y)
@@ -124,8 +124,8 @@
         for d in (2, 1, 3):
             remote(ref, ref, send_sem, recv, device(lax.rem(x + d, X), y, z, core)).start()
 
-    def across(ref):
-        remote(ref, ref, core_send, core_recv, device(x, y, z, 1 - core)).start()
+    def across(ref, recv):
+        remote(ref, ref, core_send, recv, device(x, y, z, 1 - core)).start()
 
     def part_a(xt, yt):
         return out_ref.at[rows_of(xt, yt, core, 0, A_END * ROWS)]
@@ -144,15 +144,15 @@
     wait_for(entered, (Y - 1 - y_rank) + (X - 1 - x_rank) + core)
     along_x(part_a(x, y), a_recv.at[chip])
     along_y(part_a(x, y), a_recv.at[chip])
+    lax.fori_loop(LATE, Z, swap_rest, 0)
     lax.fori_loop(A_END, LATE, swapped, 0)
     along_y(part_b(x, y), b_recv.at[chip])
     along_x(part_b(x, y), b_recv.at[chip])
-    across(early(x, y))
-    lax.fori_loop(LATE, Z, swap_rest, 0)
+    across(early(x, y), core_recv)
     lax.fori_loop(LATE, Z, swapped, 0)
     along_y(part_late(x, y), late_recv.at[chip])
     along_x(part_late(x, y), late_recv.at[chip])
-    across(part_late(x, y))
+    across(part_late(x, y), core_late)
 
     def forward(part, recv, step, over_x):
         xt, yt = (order_of(step, X), y) if over_x else (x, order_of(step, Y))
@@ -186,7 +186,7 @@
             def _():
                 waiter(part_b(xt, yt), b_recv.at[source])
 
-            across(early(xt, yt))
+            across(early(xt, yt), core_recv)
 
         return carry
 
@@ -200,14 +200,26 @@
             def _():
                 waiter(part_late(xt, yt), late_recv.at[source])
 
-            across(part_late(xt, yt))
+            across(part_late(xt, yt), core_late)
 
         return carry
 
     lax.fori_loop(0, X * Y, arrival, 0)
     lax.fori_loop(0, X * Y, late_arrival, 0)
 
-    waiter(out_ref.at[pl.ds(0, D // 2)], core_recv)
+    def largest(ct, offset, count, best):
+        def step(p, best):
+            block = jnp.abs(out_ref[pl.ds(pl.multiple_of((p * 2 + ct) * HALF + offset, ROWS), count), :])
+            return jnp.maximum(best, jnp.max(block.reshape(count // 32, 32, HEADS_WIDTH), axis=0))
+
+        return lax.fori_loop(0, X * Y, step, best, unroll=4)
+
+    best = largest(core, 0, HALF, jnp.zeros((32, HEADS_WIDTH), jnp.bfloat16))
+    waiter(out_ref.at[pl.ds(0, X * Y * LATE * ROWS)], core_recv)
+    best = largest(1 - core, 0, LATE * ROWS, best)
+    waiter(out_ref.at[pl.ds(0, X * Y * (Z - LATE) * ROWS)], core_late)
+    best = largest(1 - core, LATE * ROWS, (Z - LATE) * ROWS, best)
+    scale_ref[...] = jnp.max(best.astype(jnp.float32), axis=0, keepdims=True)
     waiter(out_ref.at[pl.ds(0, (Z - 1) * ROWS)], swap_send)
     a_rows, b_rows = A_END * ROWS, (Z - A_END) * ROWS
     sent = a_rows * ((X - 1) + X * (Y - 1)) + b_rows * ((Y - 1) + Y * (X - 1))
@@ -215,31 +227,25 @@
     waiter(out_ref.at[pl.ds(0, D // 2)], core_send)
 
 
-TILE = 1024
-
-
-def scale_kernel(w_ref, out_hbm, scale_hbm, buffer, scale_vmem, out_sem, scale_sem):
-    def step(i, best):
-        block = jnp.abs(w_ref[pl.ds(pl.multiple_of(i * 256, 256), 256), :])
-        return jnp.maximum(best, jnp.max(block.reshape(8, 32, HEADS_WIDTH), axis=0))
-
-    best = lax.fori_loop(0, D // 256, step, jnp.zeros((32, HEADS_WIDTH), jnp.bfloat16))
-    scale = jnp.max(best.astype(jnp.float32), axis=0, keepdims=True)
-    scale_vmem[...] = scale
-    scale_out = pltpu.make_async_copy(scale_vmem, scale_hbm, scale_sem)
+TILES = (512, 512, 1024, 1024, 1024, 1024, 1024, 1024, 512, 512)
+
+
+def scale_kernel(w_ref, scale_ref, out_hbm, scale_hbm, buffer, out_sem, scale_sem):
+    scale_out = pltpu.make_async_copy(scale_ref, scale_hbm, scale_sem)
     scale_out.start()
-    inverse = jnp.broadcast_to(1.0 / scale, (64, HEADS_WIDTH))
-    copies = []
-    for t in range(D // TILE):
-        def scaled(i, carry):
-            rows = pl.ds(pl.multiple_of(t * TILE + i * 64, 64), 64)
+    inverse = jnp.broadcast_to(1.0 / scale_ref[...], (64, HEADS_WIDTH))
+    copies, start = [], 0
+    for t, tile in enumerate(TILES):
+        def scaled(i, carry, start=start):
+            rows = pl.ds(pl.multiple_of(start + i * 64, 64), 64)
             buffer[rows, :] = (w_ref[rows, :].astype(jnp.float32) * inverse).astype(jnp.bfloat16)
             return carry
 
-        lax.fori_loop(0, TILE // 64, scaled, 0, unroll=4)
-        rows = pl.ds(t * TILE, TILE)
+        lax.fori_loop(0, tile // 64, scaled, 0, unroll=4)
+        rows = pl.ds(start, tile)
         copies.append(pltpu.make_async_copy(buffer.at[rows], out_hbm.at[rows], out_sem.at[t]))
         copies[-1].start()
+        start += tile
     for copy in copies:
         copy.wait()
     scale_out.wait()
@@ -247,12 +253,12 @@
 
 def shards(master_flat):
     flat = pltpu.with_memory_space_constraint(master_flat.reshape(ROWS * Z, HEADS_WIDTH), pltpu.HBM)
-    gathered = pl.pallas_call(
+    gathered, largest = pl.pallas_call(
         gather_kernel,
         name="gather",
-        out_shape=jax.ShapeDtypeStruct((D, HEADS_WIDTH), jnp.bfloat16),
+        out_shape=(jax.ShapeDtypeStruct((D, HEADS_WIDTH), jnp.bfloat16), jax.ShapeDtypeStruct((1, HEADS_WIDTH), jnp.float32)),
         in_specs=[pl.BlockSpec(memory_space=pltpu.HBM)],
-        out_specs=pl.BlockSpec(memory_space=pltpu.VMEM),
+        out_specs=(pl.BlockSpec(memory_space=pltpu.VMEM), pl.BlockSpec(memory_space=pltpu.VMEM)),
         scratch_shapes=[
             pltpu.VMEM((ROWS * Z, HEADS_WIDTH), jnp.float32),
             pltpu.VMEM((Z, ROWS, HEADS_WIDTH), jnp.bfloat16),
@@ -265,6 +271,7 @@
             pltpu.SemaphoreType.DMA((X * Y,)),
             pltpu.SemaphoreType.DMA((X * Y,)),
             pltpu.SemaphoreType.DMA((X * Y,)),
+            pltpu.SemaphoreType.DMA,
             pltpu.SemaphoreType.DMA,
             pltpu.SemaphoreType.DMA,
         ],
@@ -274,16 +281,15 @@
         scale_kernel,
         name="scale",
         out_shape=(jax.ShapeDtypeStruct((D, HEADS_WIDTH), jnp.bfloat16), jax.ShapeDtypeStruct((1, HEADS_WIDTH), jnp.float32)),
-        in_specs=[pl.BlockSpec(memory_space=pltpu.VMEM)],
+        in_specs=[pl.BlockSpec(memory_space=pltpu.VMEM), pl.BlockSpec(memory_space=pltpu.VMEM)],
         out_specs=(pl.BlockSpec(memory_space=pl.ANY), pl.BlockSpec(memory_space=pl.ANY)),
         scratch_shapes=[
             pltpu.VMEM((D, HEADS_WIDTH), jnp.bfloat16),
-            pltpu.VMEM((1, HEADS_WIDTH), jnp.float32),
-            pltpu.SemaphoreType.DMA((D // TILE,)),
+            pltpu.SemaphoreType.DMA((len(TILES),)),
             pltpu.SemaphoreType.DMA,
         ],
         compiler_params=pltpu.CompilerParams(vmem_limit_bytes=16 * 1024 * 1024),
-    )(gathered)
+    )(gathered, largest)
     return weight.reshape(1, D, HEADS_WIDTH), scale
 
 

time: 35.7 us -> 33.6 us (0.941)
  Pallas kernels: 34.9 us -> 32.8 us
    pallas_call x1, Pallas kernels: 32.6 us -> 31.3 us  [shards(): pl.pallas_call(gather_kernel, name='gather', out_shape=(jax.ShapeDtypeStr...]
    pallas_call x1, Pallas kernels: 2.3 us -> 1.45 us  [shards(): pl.pallas_call(scale_kernel, name='scale', out_shape=(jax.ShapeDtypeStruc...]
where the time goes in v4:
time: 33.6 us; the launch traced here: 33.4 us
  Pallas kernels  32.8 us (98%)
  between operations  0.64 us (2%)
    pallas_call x1, Pallas kernels, shards(): pl.pallas_call(gather_kernel, name='gather', out_shape=(jax.ShapeDtypeStr...  31.3 us
    pallas_call x1, Pallas kernels, shards(): pl.pallas_call(scale_kernel, name='scale', out_shape=(jax.ShapeDtypeStruc...  1.45 us

profile of v4, /device:TPU:1, one launch (start us, length us, event | category | flops | bytes accessed | tf_op | source)
XLA Modules:
  0.0 33.4 jit_solution(2204702787937884626)
XLA Ops:
  0.6 31.3 %gather.1 = (bf16[8192,128]{1,0:T(8,128)(2,1)S(1)}, f32[1,128]{1,0:T(1,128)S(1)}) custom-call(f32[128,128]{1,0:T(8,128)} %bitcast.2), custom_call_target="tpu_custom_call" | custom-call | tf_op jit(solution)/shard_map/gather/pallas_call | solution.py:256
  32.0 1.5 %scale.1 = (bf16[8192,128]{1,0:T(8,128)(2,1)}, f32[1,128]{1,0:T(1,128)}) custom-call(bf16[8192,128]{1,0:T(8,128)(2,1)S(1)} %get-tuple-element.6.w_ref, f32[1,128]{1,0:T(1,128)S(1)} %get-tuple-element.7.scale_ref), custom_call_target="tpu_custom_call" | custom-call | tf_op jit(solution)/shard_map/scale/pallas_call | solution.py:280

commit v5 on v4

--- a/solution.py
+++ b/solution.py
@@ -117,7 +117,7 @@
         return carry
 
     def along_y(ref, recv):
-        for d in (4, 3, 5, 2, 6, 1, 7):
+        for d in (1, 7, 2, 6, 3, 5, 4):
             remote(ref, ref, send_sem, recv, device(x, lax.rem(y + d, Y), z, core)).start()
 
     def along_x(ref, recv):
@@ -139,20 +139,22 @@
     def early(xt, yt):
         return out_ref.at[rows_of(xt, yt, core, 0, LATE * ROWS)]
 
-    lax.fori_loop(0, Z, swap_soon, 0)
-    lax.fori_loop(0, A_END, swapped, 0)
-    wait_for(entered, (Y - 1 - y_rank) + (X - 1 - x_rank) + core)
-    along_x(part_a(x, y), a_recv.at[chip])
-    along_y(part_a(x, y), a_recv.at[chip])
-    lax.fori_loop(LATE, Z, swap_rest, 0)
-    lax.fori_loop(A_END, LATE, swapped, 0)
-    along_y(part_b(x, y), b_recv.at[chip])
-    along_x(part_b(x, y), b_recv.at[chip])
-    across(early(x, y), core_recv)
-    lax.fori_loop(LATE, Z, swapped, 0)
-    along_y(part_late(x, y), late_recv.at[chip])
-    along_x(part_late(x, y), late_recv.at[chip])
-    across(part_late(x, y), core_late)
+    def own_a():
+        lax.fori_loop(0, A_END, swapped, 0)
+        along_x(part_a(x, y), a_recv.at[chip])
+        along_y(part_a(x, y), a_recv.at[chip])
+
+    def own_b():
+        lax.fori_loop(A_END, LATE, swapped, 0)
+        along_y(part_b(x, y), b_recv.at[chip])
+        along_x(part_b(x, y), b_recv.at[chip])
+        across(early(x, y), core_recv)
+
+    def own_late():
+        lax.fori_loop(LATE, Z, swapped, 0)
+        along_y(part_late(x, y), late_recv.at[chip])
+        along_x(part_late(x, y), late_recv.at[chip])
+        across(part_late(x, y), core_late)
 
     def forward(part, recv, step, over_x):
         xt, yt = (order_of(step, X), y) if over_x else (x, order_of(step, Y))
@@ -168,9 +170,33 @@
     from_x = lambda step, carry: forward(part_a, a_recv, step, True)
     from_y = lambda step, carry: forward(part_b, b_recv, step, False)
     late_from_y = lambda step, carry: forward(part_late, late_recv, step, False)
-    lax.fori_loop(0, X, from_x, 0)
-    lax.fori_loop(0, Y, from_y, 0)
-    lax.fori_loop(0, Y, late_from_y, 0)
+    def loop(start, end, body):
+        lax.fori_loop(start, end, body, 0)
+
+    loop(0, Z, swap_soon)
+
+    @pl.when(z < LATE)
+    def _():
+        wait_for(entered, (Y - 1 - y_rank) + (X - 1 - x_rank) + core)
+        own_a()
+        loop(LATE, Z, swap_rest)
+        own_b()
+        own_late()
+        loop(0, 3, from_x)
+        loop(0, Y, from_y)
+        loop(3, X, from_x)
+        loop(0, Y, late_from_y)
+
+    @pl.when(z >= LATE)
+    def _():
+        loop(LATE, Z, swap_rest)
+        wait_for(entered, (Y - 1 - y_rank) + (X - 1 - x_rank) + core)
+        own_late()
+        own_a()
+        own_b()
+        loop(0, X, from_x)
+        loop(0, Y, late_from_y)
+        loop(0, Y, from_y)
 
     def arrival(step, carry):
         xt, yt = order_of(step // 8, X), order_of(lax.rem(step, 8), Y)

time: 33.6 us -> 33.5 us (level)
  no operation moved by 1% of the time
where the time goes in v5:
time: 33.5 us; the launch traced here: 33.3 us
  Pallas kernels  32.7 us (98%)
  between operations  0.64 us (2%)
    pallas_call x1, Pallas kernels, shards(): pl.pallas_call(gather_kernel, name='gather', out_shape=(jax.ShapeDtypeStr...  31.2 us
    pallas_call x1, Pallas kernels, shards(): pl.pallas_call(scale_kernel, name='scale', out_shape=(jax.ShapeDtypeStruc...  1.45 us

profile of v5, /device:TPU:1, one launch (start us, length us, event | category | flops | bytes accessed | tf_op | source)
XLA Modules:
  0.0 33.3 jit_solution(10796498099239009220)
XLA Ops:
  0.6 31.2 %gather.1 = (bf16[8192,128]{1,0:T(8,128)(2,1)S(1)}, f32[1,128]{1,0:T(1,128)S(1)}) custom-call(f32[128,128]{1,0:T(8,128)} %bitcast.2), custom_call_target="tpu_custom_call" | custom-call | tf_op jit(solution)/shard_map/gather/pallas_call | solution.py:282
  31.8 1.5 %scale.1 = (bf16[8192,128]{1,0:T(8,128)(2,1)}, f32[1,128]{1,0:T(1,128)}) custom-call(bf16[8192,128]{1,0:T(8,128)(2,1)S(1)} %get-tuple-element.6.w_ref, f32[1,128]{1,0:T(1,128)S(1)} %get-tuple-element.7.scale_ref), custom_call_target="tpu_custom_call" | custom-call | tf_op jit(solution)/shard_map/scale/pallas_call | solution.py:306

commit v6 on v5

--- a/solution.py
+++ b/solution.py
@@ -121,7 +121,7 @@
             remote(ref, ref, send_sem, recv, device(x, lax.rem(y + d, Y), z, core)).start()
 
     def along_x(ref, recv):
-        for d in (2, 1, 3):
+        for d in (1, 3, 2):
             remote(ref, ref, send_sem, recv, device(lax.rem(x + d, X), y, z, core)).start()
 
     def across(ref, recv):
@@ -267,7 +267,7 @@
             buffer[rows, :] = (w_ref[rows, :].astype(jnp.float32) * inverse).astype(jnp.bfloat16)
             return carry
 
-        lax.fori_loop(0, tile // 64, scaled, 0, unroll=4)
+        lax.fori_loop(0, tile // 64, scaled, 0, unroll=8)
         rows = pl.ds(start, tile)
         copies.append(pltpu.make_async_copy(buffer.at[rows], out_hbm.at[rows], out_sem.at[t]))
         copies[-1].start()

time: 33.5 us -> 33.6 us (level)
  no operation moved by 1% of the time
where the time goes in v6:
time: 33.6 us; the launch traced here: 33.4 us
  Pallas kernels  32.8 us (98%)
  between operations  0.64 us (2%)
    pallas_call x1, Pallas kernels, shards(): pl.pallas_call(gather_kernel, name='gather', out_shape=(jax.ShapeDtypeStr...  31.4 us
    pallas_call x1, Pallas kernels, shards(): pl.pallas_call(scale_kernel, name='scale', out_shape=(jax.ShapeDtypeStruc...  1.43 us

profile of v6, /device:TPU:1, one launch (start us, length us, event | category | flops | bytes accessed | tf_op | source)
XLA Modules:
  0.0 33.4 jit_solution(1274485765120933785)
XLA Ops:
  0.6 31.4 %gather.1 = (bf16[8192,128]{1,0:T(8,128)(2,1)S(1)}, f32[1,128]{1,0:T(1,128)S(1)}) custom-call(f32[128,128]{1,0:T(8,128)} %bitcast.2), custom_call_target="tpu_custom_call" | custom-call | tf_op jit(solution)/shard_map/gather/pallas_call | solution.py:282
  32.0 1.4 %scale.1 = (bf16[8192,128]{1,0:T(8,128)(2,1)}, f32[1,128]{1,0:T(1,128)}) custom-call(bf16[8192,128]{1,0:T(8,128)(2,1)S(1)} %get-tuple-element.6.w_ref, f32[1,128]{1,0:T(1,128)S(1)} %get-tuple-element.7.scale_ref), custom_call_target="tpu_custom_call" | custom-call | tf_op jit(solution)/shard_map/scale/pallas_call | solution.py:306

commit v7 on v5

--- a/solution.py
+++ b/solution.py
@@ -164,6 +164,8 @@
             ref, sem = part(xt, yt), recv.at[xt * Y + yt]
             waiter(ref, sem)
             (along_y if over_x else along_x)(ref, sem)
+            if part is part_late:
+                across(ref, core_late)
 
         return 0
 
@@ -225,8 +227,7 @@
             @pl.when(xt != x)
             def _():
                 waiter(part_late(xt, yt), late_recv.at[source])
-
-            across(part_late(xt, yt), core_late)
+                across(part_late(xt, yt), core_late)
 
         return carry
 

time: 33.5 us -> 33.5 us (level)
  no operation moved by 1% of the time
where the time goes in v7:
time: 33.5 us; the launch traced here: 33.3 us
  Pallas kernels  32.7 us (98%)
  between operations  0.64 us (2%)
    pallas_call x1, Pallas kernels, shards(): pl.pallas_call(gather_kernel, name='gather', out_shape=(jax.ShapeDtypeStr...  31.2 us
    pallas_call x1, Pallas kernels, shards(): pl.pallas_call(scale_kernel, name='scale', out_shape=(jax.ShapeDtypeStruc...  1.45 us

profile of v7, /device:TPU:1, one launch (start us, length us, event | category | flops | bytes accessed | tf_op | source)
XLA Modules:
  0.0 33.3 jit_solution(9946098241604358688)
XLA Ops:
  0.6 31.2 %gather.1 = (bf16[8192,128]{1,0:T(8,128)(2,1)S(1)}, f32[1,128]{1,0:T(1,128)S(1)}) custom-call(f32[128,128]{1,0:T(8,128)} %bitcast.2), custom_call_target="tpu_custom_call" | custom-call | tf_op jit(solution)/shard_map/gather/pallas_call | solution.py:283
  31.8 1.5 %scale.1 = (bf16[8192,128]{1,0:T(8,128)(2,1)}, f32[1,128]{1,0:T(1,128)}) custom-call(bf16[8192,128]{1,0:T(8,128)(2,1)S(1)} %get-tuple-element.6.w_ref, f32[1,128]{1,0:T(1,128)S(1)} %get-tuple-element.7.scale_ref), custom_call_target="tpu_custom_call" | custom-call | tf_op jit(solution)/shard_map/scale/pallas_call | solution.py:307
